TPU v7x, 32 devices: a whole 2x2x4 slice. The times are simulated.
32 devices in a mesh: enc: 8 (over z, x), section: 2 (over core), llmdp: 2 (over y).
Axes of the slice: x: 2, y: 2, z: 4, core: 2. Of those that a mesh axis runs over, the one named last changes fastest.
Arguments:
- patches: bfloat16 [2048, 3200], P('enc', ('section', 'llmdp')), may hold values from -6 to 6
- gain: float32 [3200], replicated, may hold values from 0.25 to 1.75
- shift: float32 [3200], replicated, may hold values from -3 to 3
- proj_weight: bfloat16 [3200, 8192], P('enc', ('section', 'llmdp')), may hold values from -0.109375 to 0.109375
- llm_rank: int32 [2048, 1], P('enc'), may hold values from 0 to 7; in each aligned block of 256 rows (0 to 255, 256 to 511, ...) at most 96 rows name the same one
- embed_grad: bfloat16 [6144, 8192], P('enc', ('section', 'llmdp')), may hold values from -0.59765625 to 0.59765625
Outputs:
- embeds_recv: bfloat16 [6144, 8192], P('enc', ('section', 'llmdp'))
- hidden_state_gradient: bfloat16 [2048, 3200], P('enc', ('section', 'llmdp'))
- grad_weight: float32 [3200, 8192], P('enc', ('section', 'llmdp'))
- gain_gradient: float32 [3200], P(('section', 'llmdp'))
- grad_shift: float32 [3200], P(('section', 'llmdp'))
Inputs may be any that keep to these rules, and one draw needn't show every extreme that they name: `llm_rank`: among the 256 rows of one device, at most 96 name the same owner, a bound that some block reaches.
All inputs are finite; a program needn't handle non-finite values.
Results may differ from a plain program's by a relative error of at most 0.018.
Values may be sent and summed in bfloat16 or wider, within the bound.
A program may use at most 128 MiB of HBM per device.

v0:
```python
import jax
import jax.numpy as jnp
from jax import lax
from jax.sharding import PartitionSpec as P

EPSILON = 1e-05
MAX_BLOCK = 2


def block_size(senders, out_cols):
    size = MAX_BLOCK
    while size > 1 and (senders % size or senders == size or out_cols % (size * 128)):
        size //= 2
    return size


def body(patches, gain, shift, proj_weight, llm_rank, embed_grad):
    features = ("section", "llmdp")
    own_rows, owned_width = patches.shape
    width = gain.shape[0]
    weight_rows, out_cols = proj_weight.shape
    senders = lax.axis_size("enc")
    block = block_size(senders, out_cols)
    near = [[b * block + i for i in range(block)] for b in range(senders // block)]
    far = [[b * block + i for b in range(senders // block)] for i in range(block)]

    def near_exchange(x, split, concat):
        return lax.all_to_all(x, "enc", split, concat, axis_index_groups=near, tiled=True)

    column_start = lax.axis_index(features) * owned_width
    gain_own = lax.dynamic_slice_in_dim(gain, column_start, owned_width, 0)
    weight_part = near_exchange(proj_weight, 1, 0)
    weight = lax.all_gather(weight_part, "enc", axis=0, axis_index_groups=far, tiled=True)
    block_rows = lax.all_gather(patches, "enc", axis=0, axis_index_groups=near, tiled=True)
    complete_rows = lax.all_gather(block_rows, features, axis=1, tiled=True).astype(jnp.float32)
    row_average = jnp.mean(complete_rows, 1, keepdims=True)
    variance = jnp.mean(complete_rows * complete_rows, 1, keepdims=True) - row_average * row_average
    inverse_deviation = lax.rsqrt(variance + EPSILON)
    standardized = (complete_rows - row_average) * inverse_deviation
    normed = (standardized * gain + shift).astype(jnp.bfloat16)
    row_start = lax.axis_index("enc") % block * own_rows
    average_own = lax.dynamic_slice_in_dim(row_average, row_start, own_rows, 0)
    deviation_own = lax.dynamic_slice_in_dim(inverse_deviation, row_start, own_rows, 0)
    standardized_owned = (patches.astype(jnp.float32) - average_own) * deviation_own
    most_slots = embed_grad.shape[0] // senders
    target = llm_rank[:, 0]
    owners = jnp.arange(senders, dtype=jnp.int32)
    hits = (target[:, None] == owners[None, :]).astype(jnp.int32)
    rank = jnp.sum((jnp.cumsum(hits, 0) - hits) * hits, 1)
    slot = target * most_slots + rank

    def enc_exchange(x):
        return lax.all_to_all(
            x.reshape(senders, most_slots, out_cols), "enc", split_axis=0, concat_axis=0, tiled=True
        ).reshape(senders * most_slots, out_cols)

    d_embed = near_exchange(enc_exchange(embed_grad)[slot], 1, 0)
    grad_part = lax.psum_scatter(
        lax.dot_general(
            normed, d_embed, (((0,), (0,)), ((), ())), preferred_element_type=jnp.float32
        ).astype(jnp.bfloat16),
        "enc",
        scatter_dimension=0,
        axis_index_groups=far,
        tiled=True,
    )
    grad_weight = near_exchange(grad_part, 0, 1).astype(jnp.float32)
    embed_part = jnp.dot(normed, weight, preferred_element_type=jnp.float32).astype(jnp.bfloat16)
    embed = near_exchange(embed_part, 0, 1)
    outgoing = jnp.zeros((senders * most_slots, out_cols), jnp.bfloat16).at[slot].set(embed)
    embeds_recv = enc_exchange(outgoing)
    partial_grad = lax.dot_general(
        d_embed, weight, (((1,), (1,)), ((), ())), preferred_element_type=jnp.float32
    )
    group_count = width // owned_width
    pieces = partial_grad.astype(jnp.bfloat16).reshape(block * own_rows, group_count, owned_width)
    columns = lax.all_to_all(pieces, features, split_axis=1, concat_axis=1, tiled=True)
    column_sum = jnp.sum(columns.astype(jnp.float32), 1).astype(jnp.bfloat16)
    shares = near_exchange(column_sum.reshape(block, own_rows, owned_width), 0, 0)
    owned_normalized_gradient = jnp.sum(shares.astype(jnp.float32), 0)
    owned_centered_gradient = owned_normalized_gradient * gain_own
    mean_sum, cross_sum = lax.psum(
        (
            jnp.sum(owned_centered_gradient, 1),
            jnp.sum(owned_centered_gradient * standardized_owned, 1),
        ),
        features,
    )
    gradient_row_average = (mean_sum / width)[:, None]
    gradient_cross_product = (cross_sum / width)[:, None]
    hidden_state_gradient = (
        deviation_own
        * (
            owned_centered_gradient
            - gradient_row_average
            - standardized_owned * gradient_cross_product
        )
    ).astype(jnp.bfloat16)
    gain_gradient, grad_shift = lax.psum(
        (
            jnp.sum(owned_normalized_gradient * standardized_owned, 0),
            jnp.sum(owned_normalized_gradient, 0),
        ),
        "enc",
    )
    return (embeds_recv, hidden_state_gradient, grad_weight, gain_gradient, grad_shift)


def solution(mesh):
    in_specs = (
        P("enc", ("section", "llmdp")),
        P(),
        P(),
        P("enc", ("section", "llmdp")),
        P("enc", None),
        P("enc", ("section", "llmdp")),
    )
    out_specs = (
        P("enc", ("section", "llmdp")),
        P("enc", ("section", "llmdp")),
        P("enc", ("section", "llmdp")),
        P(("section", "llmdp")),
        P(("section", "llmdp")),
    )
    return jax.shard_map(body, mesh=mesh, in_specs=in_specs, out_specs=out_specs, check_vma=False)
```

profile of v0, /device:TPU:0, one launch (start us, length us, event | category | flops | bytes accessed | tf_op | source)
XLA Modules:
  0.0 466.7 jit_solution(16512288865410212296)
XLA Ops:
  7.2 0.0 all-gather.3.cloned.1.call-start
  7.2 15.1 %all_gather.9 = bf16[512,800]{0,1:T(8,128)(2,1)} all-gather(bf16[256,800]{0,1:T(8,128)(2,1)} %param.6), channel_id=1, replica_groups={{0,4},{8,12},{16,20},{24,28},{1,5},{9,13},{17,21},{25,29},{2,6},{10,14}..., dimensions={0}, use_global_device_ids=true | all-gather | bytes 1228800 | tf_op jit(solution)/shard_map/all_gather | solution.py:34
  22.4 0.0 all-gather.5.cloned.1.call-start
  22.4 1.6 copy.36
  24.0 23.0 %all_to_all.90 = bf16[400,2,1024]{2,0,1:T(8,128)(2,1)} all-to-all(bf16[400,2,1024]{2,0,1:T(8,128)(2,1)S(1)} %bitcast.54), channel_id=1, replica_groups={{0,4},{8,12},{16,20},{24,28},{1,5},{9,13},{17,21},{25,29},{2,6},{10,14}..., dimensions={1} | all-to-all | bytes 3276800 | tf_op jit(solution)/shard_map/all_to_all | solution.py:28
  47.0 4.9 %all-to-all-start.3 = ((bf16[8,96,2048]{2,1,0:T(8,128)(2,1)}), bf16[8,96,2048]{2,1,0:T(8,128)(2,1)S(1)}, u32[]{:S(2)}, u32[]{:S(2)}) async-start(bf16[8,96,2048]{2,1,0:T(8,128)(2,1)} %bitcast.58), calls=%async_computation.3 | async-start | bytes 6291456 | tf_op jit(solution)/shard_map/all_to_all | solution.py:53
  51.9 0.6 reduce-window.6
  52.5 0.2 slice_reduce_fusion
  52.8 0.1 fusion.8
  52.9 139.4 %all-to-all-done.3 = bf16[8,96,2048]{2,1,0:T(8,128)(2,1)S(1)} async-done(((bf16[8,96,2048]{2,1,0:T(8,128)(2,1)}), bf16[8,96,2048]{2,1,0:T(8,128)(2,1)S(1)}, u32[]{:S(2)}, u32[]{:S(2)}) %all-to-all-start.3) | async-done | bytes 3145760 | tf_op jit(solution)/shard_map/all_to_all | solution.py:53
  192.3 2.3 gather_fusion
  194.6 2.3 copy.37
  196.9 9.7 %all-to-all-start.4 = ((bf16[256,2,1024]{2,0,1:T(8,128)(2,1)}), bf16[256,2,1024]{2,0,1:T(8,128)(2,1)}, u32[]{:S(2)}, u32[]{:S(2)}) async-start(bf16[256,2,1024]{2,0,1:T(8,128)(2,1)} %bitcast.46), calls=%async_computation.4 | async-start | bytes 2097152 | tf_op jit(solution)/shard_map/all_to_all | solution.py:28
  206.6 3.0 convert_reduce_fusion
  209.6 7.6 %all-to-all-done.4 = bf16[256,2,1024]{2,0,1:T(8,128)(2,1)} async-done(((bf16[256,2,1024]{2,0,1:T(8,128)(2,1)}), bf16[256,2,1024]{2,0,1:T(8,128)(2,1)}, u32[]{:S(2)}, u32[]{:S(2)}) %all-to-all-start.4) | async-done | bytes 1048608 | tf_op jit(solution)/shard_map/all_to_all | solution.py:28
  217.2 7.5 %convolution_convert_fusion = bf16[3200,1024]{1,0:T(8,128)(2,1)} fusion(bf16[512,1024]{1,0:T(8,128)(2,1)} %bitcast.16, bf16[512,3200]{0,1:T(8,128)(2,1)S(1)} %copy-done.2, f32[3200]{0:T(1024)S(1)} %copy-done.8, f32[3200]{0:T(1024)S(1)} %copy-done.7, f32[512]{0:T(512)S(1)} %get-tuple-element.17, f32[512]{0:T(512)S(1)} %get-tuple-element.16), kind=kOutput, calls=%fused_computation.5 | convolution fusion | flops 3368550400 | bytes 10908672 | tf_op jit(solution)/shard_map/dot_general | solution.py:59
  224.8 2.2 all-gather.5.cloned.1.call-done
  227.0 6.9 %convolution_convert_fusion.1 = bf16[512,3200]{1,0:T(8,128)(2,1)S(1)} fusion(bf16[512,1024]{1,0:T(8,128)(2,1)} %bitcast.16, bf16[3200,1024]{1,0:T(8,128)(2,1)} %all-gather.5.cloned.1.call-done), kind=kOutput, calls=%fused_computation.11 | convolution fusion | flops 3357081600 | bytes 10878976 | tf_op jit(solution)/shard_map/dot_general | solution.py:72
  233.9 3.4 copy.26
  237.4 3.9 all-to-all-start.5
  241.3 8.7 %convolution_convert_fusion.2 = bf16[512,1024]{1,0:T(8,128)(2,1)} fusion(bf16[3200,1024]{1,0:T(8,128)(2,1)} %all-gather.5.cloned.1.call-done, bf16[512,3200]{0,1:T(8,128)(2,1)} %all-gather.3.cloned.1.call-done, f32[3200]{0:T(1024)S(1)} %copy-done.8, f32[3200]{0:T(1024)S(1)} %copy-done.7, f32[512]{0:T(512)S(1)} %get-tuple-element.17, ...), kind=kOutput, calls=%fused_computation.18 | convolution fusion | flops 3365797888 | bytes 10908672 | tf_op jit(solution)/shard_map/dot_general | solution.py:68
  250.0 2.3 copy.23
  252.3 27.1 %all-to-all-done.5 = bf16[512,4,800]{0,2,1:T(8,128)(2,1)S(1)} async-done(((bf16[512,4,800]{0,2,1:T(8,128)(2,1)}), bf16[512,4,800]{0,2,1:T(8,128)(2,1)S(1)}, u32[]{:S(2)}, u32[]{:S(2)}) %all-to-all-start.5) | async-done | bytes 3276832 | tf_op jit(solution)/shard_map/all_to_all | solution.py:77
  279.4 4.4 all-to-all-start.1
  283.8 1.6 reduce_sum.90
  285.4 2.1 copy.38
  287.5 10.1 %all-to-all-done.1 = bf16[2,256,1024]{1,2,0:T(8,128)(2,1)} async-done(((bf16[2,256,1024]{1,2,0:T(8,128)(2,1)}), bf16[2,256,1024]{1,2,0:T(8,128)(2,1)}, u32[]{:S(2)}, u32[]{:S(2)}) %all-to-all-start.1) | async-done | bytes 1048608 | tf_op jit(solution)/shard_map/all_to_all | solution.py:28
  297.6 3.5 all-to-all-start.6
  301.1 1.5 copy.24
  302.6 4.3 scatter_custom_fusion
  306.9 4.6 all-to-all-done.6
  311.5 0.9 copy-done.3
  312.4 9.3 %all-to-all-start.2 = ((bf16[8,96,2048]{2,1,0:T(8,128)(2,1)}), bf16[8,96,2048]{2,1,0:T(8,128)(2,1)S(1)}, u32[]{:S(2)}, u32[]{:S(2)}) async-start(bf16[8,96,2048]{2,1,0:T(8,128)(2,1)} %bitcast.52), calls=%async_computation.2 | async-start | bytes 6291456 | tf_op jit(solution)/shard_map/all_to_all | solution.py:53
  321.7 1.4 dynamic_slice.8
  323.1 1.3 dynamic-slice.3
  324.4 1.3 dynamic-slice.4
  325.8 87.7 %all-to-all-done.2 = bf16[8,96,2048]{2,1,0:T(8,128)(2,1)S(1)} async-done(((bf16[8,96,2048]{2,1,0:T(8,128)(2,1)}), bf16[8,96,2048]{2,1,0:T(8,128)(2,1)S(1)}, u32[]{:S(2)}, u32[]{:S(2)}) %all-to-all-start.2) | async-done | bytes 3145760 | tf_op jit(solution)/shard_map/all_to_all | solution.py:53
  413.5 4.6 all-to-all-start.7
  418.2 2.0 convert_reduce_fusion.1
  420.2 0.9 copy-done
  421.1 1.7 multiply_reduce_fusion
  422.8 8.2 %all-reduce.1 = (f32[256]{0:T(256)}, f32[256]{0:T(256)}) all-reduce(f32[256]{0:T(256)} %get-tuple-element.8, f32[256]{0:T(256)} %get-tuple-element.9), channel_id=1, replica_groups=mesh['enc'=8,'section'=2,'llmdp'=2] {'section','llmdp'}, use_global_device_ids=true, to_apply=%region_11.12 | all-reduce | flops 512 | bytes 4096 | tf_op jit(solution)/shard_map/psum | solution.py:82
  431.0 20.9 %all-reduce = (f32[800]{0:T(1024)}, f32[800]{0:T(1024)}) all-reduce(f32[800]{0:T(1024)} %get-tuple-element.7, f32[800]{0:T(1024)} %get-tuple-element.10), channel_id=1, replica_groups=mesh['enc'=8,'section'=2,'llmdp'=2] {'enc'}, use_global_device_ids=true, to_apply=%region_14.15 | all-reduce | flops 1600 | bytes 12800 | tf_op jit(solution)/shard_map/psum | solution.py:99
  451.9 0.7 broadcast_multiply_fusion.1
  452.6 2.1 multiply_convert_fusion
  454.7 1.8 convert_bitcast_fusion
  456.5 1.9 copy.32
  458.5 1.7 copy.40
  (29 shorter events, 0.2 us)
Async XLA Ops:
  7.2 199.4 %all-gather.3.cloned.1.call-start = ((), (), s32[]{:S(2)}) async-start(), calls=%async_computation.9 | async-start | bytes 4096000 | tf_op jit(solution)/shard_map/all_gather | solution.py:35
  22.4 204.6 %all-gather.5.cloned.1.call-start = ((), (), s32[]{:S(2)}) async-start(), calls=%async_computation.10 | async-start | bytes 8192000 | tf_op jit(solution)/shard_map/all_gather | solution.py:33
  47.0 4.9 %copy-start.4 = (s32[256,1]{0,1:T(1,128)S(1)}, s32[256,1]{0,1:T(1,128)}, u32[]{:S(2)}) copy-start(s32[256,1]{0,1:T(1,128)} %param.10) | copy-start | bytes 3076
  47.0 145.3 %all-to-all-start.3 = ((bf16[8,96,2048]{2,1,0:T(8,128)(2,1)}), bf16[8,96,2048]{2,1,0:T(8,128)(2,1)S(1)}, u32[]{:S(2)}, u32[]{:S(2)}) async-start(bf16[8,96,2048]{2,1,0:T(8,128)(2,1)} %bitcast.58), calls=%async_computation.3 | async-start | bytes 6291456 | tf_op jit(solution)/shard_map/all_to_all | solution.py:53
  194.6 22.6 %copy-start.7 = (f32[3200]{0:T(1024)S(1)}, f32[3200]{0:T(1024)}, u32[]{:S(2)}) copy-start(f32[3200]{0:T(1024)} %param.7) | copy-start | bytes 38404
  194.6 22.6 %copy-start.8 = (f32[3200]{0:T(1024)S(1)}, f32[3200]{0:T(1024)}, u32[]{:S(2)}) copy-start(f32[3200]{0:T(1024)} %param.8) | copy-start | bytes 38404
  196.9 20.3 %all-to-all-start.4 = ((bf16[256,2,1024]{2,0,1:T(8,128)(2,1)}), bf16[256,2,1024]{2,0,1:T(8,128)(2,1)}, u32[]{:S(2)}, u32[]{:S(2)}) async-start(bf16[256,2,1024]{2,0,1:T(8,128)(2,1)} %bitcast.46), calls=%async_computation.4 | async-start | bytes 2097152 | tf_op jit(solution)/shard_map/all_to_all | solution.py:28
  206.6 206.9 %reduce-scatter.2.cloned.1.call-start = ((), (), s32[]{:S(2)}) async-start(), calls=%async_computation.11 | async-start | bytes 8192000 | tf_op jit(solution)/shard_map/reduce_scatter | solution.py:58
  206.6 10.6 %copy-start.2 = (bf16[512,3200]{0,1:T(8,128)(2,1)S(1)}, bf16[512,3200]{0,1:T(8,128)(2,1)}, u32[]{:S(2)}) copy-start(bf16[512,3200]{0,1:T(8,128)(2,1)} %all-gather.3.cloned.1.call-done) | copy-start | bytes 9830404
  209.6 31.7 %copy-start.5 = (f32[512]{0:T(512)}, f32[512]{0:T(512)S(1)}, u32[]{:S(2)}) copy-start(f32[512]{0:T(512)S(1)} %get-tuple-element.17) | copy-start | bytes 6148
  209.6 31.7 %copy-start.6 = (f32[512]{0:T(512)}, f32[512]{0:T(512)S(1)}, u32[]{:S(2)}) copy-start(f32[512]{0:T(512)S(1)} %get-tuple-element.16) | copy-start | bytes 6148
  237.4 42.0 %all-to-all-start.5 = ((bf16[512,4,800]{0,2,1:T(8,128)(2,1)}), bf16[512,4,800]{0,2,1:T(8,128)(2,1)S(1)}, u32[]{:S(2)}, u32[]{:S(2)}) async-start(bf16[512,4,800]{0,2,1:T(8,128)(2,1)} %bitcast.50), calls=%async_computation.5 | async-start | bytes 6553600 | tf_op jit(solution)/shard_map/all_to_all | solution.py:77
  279.4 18.2 %all-to-all-start.1 = ((bf16[2,256,1024]{1,2,0:T(8,128)(2,1)}), bf16[2,256,1024]{1,2,0:T(8,128)(2,1)}, u32[]{:S(2)}, u32[]{:S(2)}) async-start(bf16[2,256,1024]{1,2,0:T(8,128)(2,1)} %copy.23), calls=%async_computation.1 | async-start | bytes 2097152 | tf_op jit(solution)/shard_map/all_to_all | solution.py:28
  297.6 13.9 %all-to-all-start.6 = ((bf16[2,256,800]{1,2,0:T(8,128)(2,1)}), bf16[2,256,800]{1,2,0:T(8,128)(2,1)S(1)}, u32[]{:S(2)}, u32[]{:S(2)}) async-start(bf16[2,256,800]{1,2,0:T(8,128)(2,1)} %bitcast.47), calls=%async_computation.6 | async-start | bytes 1638400 | tf_op jit(solution)/shard_map/all_to_all | solution.py:28
  311.5 0.9 copy-start.3
  312.4 101.1 %all-to-all-start.2 = ((bf16[8,96,2048]{2,1,0:T(8,128)(2,1)}), bf16[8,96,2048]{2,1,0:T(8,128)(2,1)S(1)}, u32[]{:S(2)}, u32[]{:S(2)}) async-start(bf16[8,96,2048]{2,1,0:T(8,128)(2,1)} %bitcast.52), calls=%async_computation.2 | async-start | bytes 6291456 | tf_op jit(solution)/shard_map/all_to_all | solution.py:53
  321.7 99.4 %copy-start.1 = (bf16[256,800]{0,1:T(8,128)(2,1)S(1)}, bf16[256,800]{0,1:T(8,128)(2,1)}, u32[]{:S(2)}) copy-start(bf16[256,800]{0,1:T(8,128)(2,1)} %param.6) | copy-start | bytes 1228804
  413.5 41.2 %all-to-all-start.7 = ((bf16[2,400,1024]{2,1,0:T(8,128)(2,1)}), bf16[2,400,1024]{2,1,0:T(8,128)(2,1)}, u32[]{:S(2)}, u32[]{:S(2)}) async-start(bf16[2,400,1024]{2,1,0:T(8,128)(2,1)} %bitcast.60), calls=%async_computation.8 | async-start | bytes 3276800 | tf_op jit(solution)/shard_map/all_to_all | solution.py:28
  420.2 0.9 copy-start
Sparse Core Ops, SparseCore 0:
  22.5 29.5 all-gather.2
  53.7 173.2 all-gather.4
  229.3 138.2 reduce-scatter.1
where the time goes:
time: 468 us; the launch traced here: 467 us
  waiting for transfers between devices  279 us (60%)
  blocking collectives  67.3 us (14%)
  starting transfers between devices  40.5 us (9%)
  local copies, waits for them, and re-layouts  29.5 us (6%)
  matrix products  23.1 us (5%)
  between operations  13.9 us (3%)
  other arithmetic  13.7 us (3%)
    all_to_all x2, waiting for transfers between devices, enc_exchange(): lax.all_to_all(x.reshape(senders, most_slots, out_cols), 'enc', split_axi...  227 us
    all_to_all x1, waiting for transfers between devices, body(): lax.all_to_all(pieces, features, split_axis=1, concat_axis=1, tiled=True)  27.1 us
    all_to_all x1, blocking collectives, near_exchange(): lax.all_to_all(x, 'enc', split, concat, axis_index_groups=near, tiled=True)  23 us
    all_to_all x4, starting transfers between devices, near_exchange(): lax.all_to_all(x, 'enc', split, concat, axis_index_groups=near, tiled=True)  22.3 us
    all_to_all x4, waiting for transfers between devices, near_exchange(): lax.all_to_all(x, 'enc', split, concat, axis_index_groups=near, tiled=True)  22.2 us
    psum x1, blocking collectives, body(): lax.psum((jnp.sum(owned_normalized_gradient * standardized_owned, 0), jnp...  20.9 us
    all_gather x1, blocking collectives, body(): lax.all_gather(patches, 'enc', axis=0, axis_index_groups=near, tiled=True)  15.1 us
    all_to_all x2, starting transfers between devices, enc_exchange(): lax.all_to_all(x.reshape(senders, most_slots, out_cols), 'enc', split_axi...  14.2 us
  transfers between devices with their start and end apart: 10, of which 7 were waited for; matrix products, arithmetic and copies ran while one was open for 13% of the time, Pallas kernels for 0%

commit v1 on v0

--- a/solution.py
+++ b/solution.py
@@ -74,7 +74,12 @@
     )
     group_count = width // owned_width
     pieces = partial_grad.astype(jnp.bfloat16).reshape(block * own_rows, group_count, owned_width)
-    columns = lax.all_to_all(pieces, features, split_axis=1, concat_axis=1, tiled=True)
+    columns = jnp.concatenate(
+        lax.all_to_all(
+            jnp.stack(jnp.split(pieces, lax.axis_size(features), axis=1)), features, 0, 0
+        ),
+        axis=1,
+    )
     column_sum = jnp.sum(columns.astype(jnp.float32), 1).astype(jnp.bfloat16)
     shares = near_exchange(column_sum.reshape(block, own_rows, owned_width), 0, 0)
     owned_normalized_gradient = jnp.sum(shares.astype(jnp.float32), 0)

time: 468 us -> 468 us (level)
  waiting for transfers between devices: 279 us -> 274 us
  transfers between devices with their start and end apart: 10 -> 10, of which waited for: 7 -> 7; matrix products, arithmetic and copies ran while one was open for 13% -> 14% of each run, Pallas kernels for 0% -> 0%
where the time goes in v1:
time: 468 us; the launch traced here: 467 us
  waiting for transfers between devices  274 us (59%)
  blocking collectives  67.3 us (14%)
  starting transfers between devices  40.1 us (9%)
  local copies, waits for them, and re-layouts  30.7 us (7%)
  matrix products  24.8 us (5%)
  other arithmetic  15.6 us (3%)
  between operations  13.9 us (3%)
    all_to_all x2, waiting for transfers between devices, enc_exchange(): lax.all_to_all(x.reshape(senders, most_slots, out_cols), 'enc', split_axi...  223 us
    all_to_all x1, waiting for transfers between devices, body(): lax.all_to_all(jnp.stack(jnp.split(pieces, lax.axis_size(features), axis=...  27.1 us
    all_to_all x1, blocking collectives, near_exchange(): lax.all_to_all(x, 'enc', split, concat, axis_index_groups=near, tiled=True)  23 us
    all_to_all x4, starting transfers between devices, near_exchange(): lax.all_to_all(x, 'enc', split, concat, axis_index_groups=near, tiled=True)  22.3 us
    all_to_all x4, waiting for transfers between devices, near_exchange(): lax.all_to_all(x, 'enc', split, concat, axis_index_groups=near, tiled=True)  22.2 us
    psum x1, blocking collectives, body(): lax.psum((jnp.sum(owned_normalized_gradient * standardized_owned, 0), jnp...  20.9 us
    all_gather x1, blocking collectives, body(): lax.all_gather(patches, 'enc', axis=0, axis_index_groups=near, tiled=True)  15.1 us
    all_to_all x2, starting transfers between devices, enc_exchange(): lax.all_to_all(x.reshape(senders, most_slots, out_cols), 'enc', split_axi...  13.9 us
  transfers between devices with their start and end apart: 10, of which 7 were waited for; matrix products, arithmetic and copies ran while one was open for 14% of the time, Pallas kernels for 0%

profile of v1, /device:TPU:0, one launch (start us, length us, event | category | flops | bytes accessed | tf_op | source)
XLA Modules:
  0.0 466.7 jit_solution(10899816472604331814)
XLA Ops:
  7.2 15.1 %all_gather.9 = bf16[512,800]{0,1:T(8,128)(2,1)} all-gather(bf16[256,800]{0,1:T(8,128)(2,1)} %param.6), channel_id=1, replica_groups={{0,4},{8,12},{16,20},{24,28},{1,5},{9,13},{17,21},{25,29},{2,6},{10,14}..., dimensions={0}, use_global_device_ids=true | all-gather | bytes 1228800 | tf_op jit(solution)/shard_map/all_gather | solution.py:34
  22.4 1.6 copy.39
  24.0 23.0 %all_to_all.90 = bf16[400,2,1024]{2,0,1:T(8,128)(2,1)} all-to-all(bf16[400,2,1024]{2,0,1:T(8,128)(2,1)S(1)} %bitcast.62), channel_id=1, replica_groups={{0,4},{8,12},{16,20},{24,28},{1,5},{9,13},{17,21},{25,29},{2,6},{10,14}..., dimensions={1} | all-to-all | bytes 3276800 | tf_op jit(solution)/shard_map/all_to_all | solution.py:28
  47.0 4.9 %all-to-all-start.3 = ((bf16[8,96,2048]{2,1,0:T(8,128)(2,1)}), bf16[8,96,2048]{2,1,0:T(8,128)(2,1)S(1)}, u32[]{:S(2)}, u32[]{:S(2)}) async-start(bf16[8,96,2048]{2,1,0:T(8,128)(2,1)} %bitcast.66), calls=%async_computation.3 | async-start | bytes 6291456 | tf_op jit(solution)/shard_map/all_to_all | solution.py:53
  51.9 0.6 reduce-window.6
  52.5 0.2 slice_reduce_fusion
  52.8 0.1 fusion.8
  52.9 139.4 %all-to-all-done.3 = bf16[8,96,2048]{2,1,0:T(8,128)(2,1)S(1)} async-done(((bf16[8,96,2048]{2,1,0:T(8,128)(2,1)}), bf16[8,96,2048]{2,1,0:T(8,128)(2,1)S(1)}, u32[]{:S(2)}, u32[]{:S(2)}) %all-to-all-start.3) | async-done | bytes 3145760 | tf_op jit(solution)/shard_map/all_to_all | solution.py:53
  192.3 2.3 gather_fusion
  194.6 2.3 copy.40
  196.9 9.7 %all-to-all-start.4 = ((bf16[256,2,1024]{2,0,1:T(8,128)(2,1)}), bf16[256,2,1024]{2,0,1:T(8,128)(2,1)}, u32[]{:S(2)}, u32[]{:S(2)}) async-start(bf16[256,2,1024]{2,0,1:T(8,128)(2,1)} %bitcast.54), calls=%async_computation.4 | async-start | bytes 2097152 | tf_op jit(solution)/shard_map/all_to_all | solution.py:28
  206.6 3.0 convert_reduce_fusion
  209.6 7.6 %all-to-all-done.4 = bf16[256,2,1024]{2,0,1:T(8,128)(2,1)} async-done(((bf16[256,2,1024]{2,0,1:T(8,128)(2,1)}), bf16[256,2,1024]{2,0,1:T(8,128)(2,1)}, u32[]{:S(2)}, u32[]{:S(2)}) %all-to-all-start.4) | async-done | bytes 1048608 | tf_op jit(solution)/shard_map/all_to_all | solution.py:28
  217.2 7.5 %convolution_convert_fusion = bf16[3200,1024]{1,0:T(8,128)(2,1)} fusion(bf16[512,1024]{1,0:T(8,128)(2,1)} %bitcast.16, bf16[512,3200]{0,1:T(8,128)(2,1)S(1)} %copy-done.2, f32[3200]{0:T(1024)S(1)} %copy-done.8, f32[3200]{0:T(1024)S(1)} %copy-done.7, f32[512]{0:T(512)S(1)} %get-tuple-element.21, f32[512]{0:T(512)S(1)} %get-tuple-element.20), kind=kOutput, calls=%fused_computation.5 | convolution fusion | flops 3368550400 | bytes 10908672 | tf_op jit(solution)/shard_map/dot_general | solution.py:59
  224.8 2.2 all-gather.5.cloned.1.call-done
  227.0 8.6 %convolution_convert_fusion.1 = bf16[512,3200]{1,0:T(8,128)(2,1)} fusion(bf16[512,1024]{1,0:T(8,128)(2,1)} %bitcast.16, bf16[3200,1024]{1,0:T(8,128)(2,1)} %all-gather.5.cloned.1.call-done), kind=kOutput, calls=%fused_computation.11 | convolution fusion | flops 3357081600 | bytes 10878976 | tf_op jit(solution)/shard_map/dot_general | solution.py:72
  235.6 4.4 copy.29
  240.0 0.2 slice_bitcast_fusion.3
  240.3 1.9 pad_maximum_fusion
  242.2 3.9 all-to-all-start.5
  246.1 8.7 %convolution_convert_fusion.2 = bf16[512,1024]{1,0:T(8,128)(2,1)} fusion(bf16[3200,1024]{1,0:T(8,128)(2,1)} %all-gather.5.cloned.1.call-done, bf16[512,3200]{0,1:T(8,128)(2,1)} %all-gather.3.cloned.1.call-done, f32[3200]{0:T(1024)S(1)} %copy-done.8, f32[3200]{0:T(1024)S(1)} %copy-done.7, f32[512]{0:T(512)S(1)} %get-tuple-element.21, ...), kind=kOutput, calls=%fused_computation.19 | convolution fusion | flops 3365797888 | bytes 10908672 | tf_op jit(solution)/shard_map/dot_general | solution.py:68
  254.8 2.3 copy.26
  257.1 27.1 %all-to-all-done.5 = bf16[4,512,1,800]{1,3,2,0:T(8,128)(2,1)S(1)} async-done(((bf16[4,512,1,800]{1,3,2,0:T(8,128)(2,1)}), bf16[4,512,1,800]{1,3,2,0:T(8,128)(2,1)S(1)}, u32[]{:S(2)}, u32[]{:S(2)}) %all-to-all-start.5) | async-done | bytes 3276832 | tf_op jit(solution)/shard_map/all_to_all | solution.py:78
  284.2 4.4 all-to-all-start.1
  288.6 1.6 reduce_sum.90
  290.2 2.1 copy.41
  292.3 10.1 %all-to-all-done.1 = bf16[2,256,1024]{1,2,0:T(8,128)(2,1)} async-done(((bf16[2,256,1024]{1,2,0:T(8,128)(2,1)}), bf16[2,256,1024]{1,2,0:T(8,128)(2,1)}, u32[]{:S(2)}, u32[]{:S(2)}) %all-to-all-start.1) | async-done | bytes 1048608 | tf_op jit(solution)/shard_map/all_to_all | solution.py:28
  302.4 3.5 all-to-all-start.6
  305.9 1.5 copy.27
  307.4 4.3 scatter_custom_fusion
  311.7 4.6 all-to-all-done.6
  316.3 0.9 copy-done.3
  317.2 9.0 %all-to-all-start.2 = ((bf16[8,96,2048]{2,1,0:T(8,128)(2,1)}), bf16[8,96,2048]{2,1,0:T(8,128)(2,1)S(1)}, u32[]{:S(2)}, u32[]{:S(2)}) async-start(bf16[8,96,2048]{2,1,0:T(8,128)(2,1)} %bitcast.60), calls=%async_computation.2 | async-start | bytes 6291456 | tf_op jit(solution)/shard_map/all_to_all | solution.py:53
  326.2 1.4 dynamic_slice.8
  327.6 1.3 dynamic-slice.3
  328.9 1.3 dynamic-slice.4
  330.2 83.3 %all-to-all-done.2 = bf16[8,96,2048]{2,1,0:T(8,128)(2,1)S(1)} async-done(((bf16[8,96,2048]{2,1,0:T(8,128)(2,1)}), bf16[8,96,2048]{2,1,0:T(8,128)(2,1)S(1)}, u32[]{:S(2)}, u32[]{:S(2)}) %all-to-all-start.2) | async-done | bytes 3145760 | tf_op jit(solution)/shard_map/all_to_all | solution.py:53
  413.5 4.6 all-to-all-start.7
  418.2 2.0 convert_reduce_fusion.1
  420.2 0.9 copy-done
  421.1 1.7 multiply_reduce_fusion
  422.8 8.2 %all-reduce.1 = (f32[256]{0:T(256)}, f32[256]{0:T(256)}) all-reduce(f32[256]{0:T(256)} %get-tuple-element.8, f32[256]{0:T(256)} %get-tuple-element.9), channel_id=1, replica_groups=mesh['enc'=8,'section'=2,'llmdp'=2] {'section','llmdp'}, use_global_device_ids=true, to_apply=%region_11.12 | all-reduce | flops 512 | bytes 4096 | tf_op jit(solution)/shard_map/psum | solution.py:87
  431.0 20.9 %all-reduce = (f32[800]{0:T(1024)}, f32[800]{0:T(1024)}) all-reduce(f32[800]{0:T(1024)} %get-tuple-element.7, f32[800]{0:T(1024)} %get-tuple-element.10), channel_id=1, replica_groups=mesh['enc'=8,'section'=2,'llmdp'=2] {'enc'}, use_global_device_ids=true, to_apply=%region_14.15 | all-reduce | flops 1600 | bytes 12800 | tf_op jit(solution)/shard_map/psum | solution.py:104
  451.9 0.7 broadcast_multiply_fusion.1
  452.6 2.1 multiply_convert_fusion
  454.7 1.8 convert_bitcast_fusion
  456.6 1.9 copy.35
  458.5 1.7 copy.43
  (31 shorter events, 0.2 us)
Async XLA Ops:
  7.2 199.4 %all-gather.3.cloned.1.call-start = ((), (), s32[]{:S(2)}) async-start(), calls=%async_computation.9 | async-start | bytes 4096000 | tf_op jit(solution)/shard_map/all_gather | solution.py:35
  22.4 204.6 %all-gather.5.cloned.1.call-start = ((), (), s32[]{:S(2)}) async-start(), calls=%async_computation.10 | async-start | bytes 8192000 | tf_op jit(solution)/shard_map/all_gather | solution.py:33
  47.0 4.9 %copy-start.4 = (s32[256,1]{0,1:T(1,128)S(1)}, s32[256,1]{0,1:T(1,128)}, u32[]{:S(2)}) copy-start(s32[256,1]{0,1:T(1,128)} %param.10) | copy-start | bytes 3076
  47.0 145.3 %all-to-all-start.3 = ((bf16[8,96,2048]{2,1,0:T(8,128)(2,1)}), bf16[8,96,2048]{2,1,0:T(8,128)(2,1)S(1)}, u32[]{:S(2)}, u32[]{:S(2)}) async-start(bf16[8,96,2048]{2,1,0:T(8,128)(2,1)} %bitcast.66), calls=%async_computation.3 | async-start | bytes 6291456 | tf_op jit(solution)/shard_map/all_to_all | solution.py:53
  194.6 22.6 %copy-start.7 = (f32[3200]{0:T(1024)S(1)}, f32[3200]{0:T(1024)}, u32[]{:S(2)}) copy-start(f32[3200]{0:T(1024)} %param.7) | copy-start | bytes 38404
  194.6 22.6 %copy-start.8 = (f32[3200]{0:T(1024)S(1)}, f32[3200]{0:T(1024)}, u32[]{:S(2)}) copy-start(f32[3200]{0:T(1024)} %param.8) | copy-start | bytes 38404
  196.9 20.3 %all-to-all-start.4 = ((bf16[256,2,1024]{2,0,1:T(8,128)(2,1)}), bf16[256,2,1024]{2,0,1:T(8,128)(2,1)}, u32[]{:S(2)}, u32[]{:S(2)}) async-start(bf16[256,2,1024]{2,0,1:T(8,128)(2,1)} %bitcast.54), calls=%async_computation.4 | async-start | bytes 2097152 | tf_op jit(solution)/shard_map/all_to_all | solution.py:28
  206.6 206.9 %reduce-scatter.2.cloned.1.call-start = ((), (), s32[]{:S(2)}) async-start(), calls=%async_computation.11 | async-start | bytes 8192000 | tf_op jit(solution)/shard_map/reduce_scatter | solution.py:58
  206.6 10.6 %copy-start.2 = (bf16[512,3200]{0,1:T(8,128)(2,1)S(1)}, bf16[512,3200]{0,1:T(8,128)(2,1)}, u32[]{:S(2)}) copy-start(bf16[512,3200]{0,1:T(8,128)(2,1)} %all-gather.3.cloned.1.call-done) | copy-start | bytes 9830404
  209.6 36.5 %copy-start.5 = (f32[512]{0:T(512)}, f32[512]{0:T(512)S(1)}, u32[]{:S(2)}) copy-start(f32[512]{0:T(512)S(1)} %get-tuple-element.21) | copy-start | bytes 6148
  209.6 36.5 %copy-start.6 = (f32[512]{0:T(512)}, f32[512]{0:T(512)S(1)}, u32[]{:S(2)}) copy-start(f32[512]{0:T(512)S(1)} %get-tuple-element.20) | copy-start | bytes 6148
  242.2 42.0 %all-to-all-start.5 = ((bf16[4,512,1,800]{1,3,2,0:T(8,128)(2,1)}), bf16[4,512,1,800]{1,3,2,0:T(8,128)(2,1)S(1)}, u32[]{:S(2)}, u32[]{:S(2)}) async-start(bf16[4,512,1,800]{1,3,2,0:T(8,128)(2,1)} %pad_maximum_fusion), calls=%async_computation.5 | async-start | bytes 6553600 | tf_op jit(solution)/shard_map/all_to_all | solution.py:78
  284.2 18.2 %all-to-all-start.1 = ((bf16[2,256,1024]{1,2,0:T(8,128)(2,1)}), bf16[2,256,1024]{1,2,0:T(8,128)(2,1)}, u32[]{:S(2)}, u32[]{:S(2)}) async-start(bf16[2,256,1024]{1,2,0:T(8,128)(2,1)} %copy.26), calls=%async_computation.1 | async-start | bytes 2097152 | tf_op jit(solution)/shard_map/all_to_all | solution.py:28
  302.4 13.9 %all-to-all-start.6 = ((bf16[2,256,800]{1,2,0:T(8,128)(2,1)}), bf16[2,256,800]{1,2,0:T(8,128)(2,1)S(1)}, u32[]{:S(2)}, u32[]{:S(2)}) async-start(bf16[2,256,800]{1,2,0:T(8,128)(2,1)} %bitcast.55), calls=%async_computation.6 | async-start | bytes 1638400 | tf_op jit(solution)/shard_map/all_to_all | solution.py:28
  316.3 0.9 copy-start.3
  317.2 96.3 %all-to-all-start.2 = ((bf16[8,96,2048]{2,1,0:T(8,128)(2,1)}), bf16[8,96,2048]{2,1,0:T(8,128)(2,1)S(1)}, u32[]{:S(2)}, u32[]{:S(2)}) async-start(bf16[8,96,2048]{2,1,0:T(8,128)(2,1)} %bitcast.60), calls=%async_computation.2 | async-start | bytes 6291456 | tf_op jit(solution)/shard_map/all_to_all | solution.py:53
  326.2 94.9 %copy-start.1 = (bf16[256,800]{0,1:T(8,128)(2,1)S(1)}, bf16[256,800]{0,1:T(8,128)(2,1)}, u32[]{:S(2)}) copy-start(bf16[256,800]{0,1:T(8,128)(2,1)} %param.6) | copy-start | bytes 1228804
  413.5 41.2 %all-to-all-start.7 = ((bf16[2,400,1024]{2,1,0:T(8,128)(2,1)}), bf16[2,400,1024]{2,1,0:T(8,128)(2,1)}, u32[]{:S(2)}, u32[]{:S(2)}) async-start(bf16[2,400,1024]{2,1,0:T(8,128)(2,1)} %bitcast.68), calls=%async_computation.8 | async-start | bytes 3276800 | tf_op jit(solution)/shard_map/all_to_all | solution.py:28
  420.2 0.9 copy-start
Sparse Core Ops, SparseCore 0:
  22.5 29.5 all-gather.2
  53.7 173.2 all-gather.4
  229.3 133.9 reduce-scatter.1
